TPU v7x, 32 devices: a whole 2x2x4 slice. The times are simulated.
32 devices in a mesh: lat: 4 (over y, x), lon: 8 (over z, core).
Axes of the slice: x: 2, y: 2, z: 4, core: 2. Of those that a mesh axis runs over, the one named last changes fastest.
Arguments:
- latent_field: bfloat16 [640, 32, 64], P(None, 'lat', 'lon'), may hold values from -6 to 6
- spectral_filter: float32 [640, 32], P('lon'), may hold values from -5 to 5
- conv_weight: float32 [9, 640], replicated, may hold values from -2 to 2
- norm_gain: float32 [640], replicated, may hold values from 0.1 to 1.9
- weight_in: bfloat16 [640, 1280], replicated, may hold values from -0.25 to 0.25
- weight_out: bfloat16 [1280, 640], replicated, may hold values from -0.15625 to 0.15625
Outputs:
- updated: bfloat16 [640, 32, 64], P(None, 'lat', 'lon')
All inputs are finite; a program needn't handle non-finite values.
Results may differ from a plain program's by a relative error of at most 0.01.
Values may be sent and summed in bfloat16 or wider, within the bound.
A program may use at most 128 MiB of HBM per device.

v0:
```python
import functools
import math
import jax
import jax.numpy as jnp
import numpy as np
from jax import lax
from jax.sharding import PartitionSpec as P

highest = lax.Precision.HIGHEST
epsilon_norm = 1e-06


def with_halo(cells, sides, width):
    for axis, dim in sides:
        count = lax.axis_size(axis)
        ends = count - 1
        head = lax.slice_in_dim(cells, 0, width, axis=dim)
        tail = lax.slice_in_dim(cells, cells.shape[dim] - width, cells.shape[dim], axis=dim)
        cells = jnp.concatenate(
            [
                lax.ppermute(tail, axis, [(i, (i + 1) % count) for i in range(ends)]),
                cells,
                lax.ppermute(head, axis, [((i + 1) % count, i) for i in range(ends)]),
            ],
            axis=dim,
        )
    return cells


def quadrature(lat_count):
    colatitude = (jnp.arange(lat_count, dtype=jnp.float32) + 0.5) * (math.pi / lat_count)
    return jnp.sin(colatitude) * (math.pi / lat_count)


def fourier_tables(lon_count, mode_count):
    wave_index = (
        jnp.arange(mode_count, dtype=jnp.int32)[:, None]
        * jnp.arange(lon_count, dtype=jnp.int32)[None, :]
    )
    phase_angle = (wave_index % lon_count).astype(jnp.float32) * (2.0 * math.pi / lon_count)
    cosine = jnp.cos(phase_angle)
    sine_table = jnp.sin(phase_angle)
    angle_step = 2.0 * math.pi / lon_count
    forward = jnp.concatenate([angle_step * cosine, -angle_step * sine_table], axis=0)
    weight = jnp.where(jnp.arange(mode_count, dtype=jnp.int32) == 0, 1.0, 2.0).astype(jnp.float32)[
        :, None
    ]
    inverse = jnp.concatenate([weight * cosine, -weight * sine_table], axis=0)
    return (forward, inverse)


def legendre_rows(order_ids, lat_count):
    colatitude = (jnp.arange(lat_count, dtype=jnp.float32) + 0.5) * (math.pi / lat_count)
    cosine = jnp.cos(colatitude)
    sine_col = jnp.sin(colatitude)
    order_f = order_ids.astype(jnp.float32)
    factor_index = jnp.arange(1, lat_count, dtype=jnp.float32)
    ratio_log = jnp.log((2.0 * factor_index - 1.0) / (2.0 * factor_index))
    included = (factor_index[None, :] <= order_f[:, None]).astype(jnp.float32)
    log_factor = jnp.sum(included * ratio_log[None, :], axis=1)
    start_log = 0.5 * jnp.log((2.0 * order_f + 1.0) / (4.0 * math.pi)) + 0.5 * log_factor
    start_log = start_log[:, None] + order_f[:, None] * jnp.log(sine_col)[None, :]
    blank_rows = jnp.zeros((order_ids.shape[0], lat_count), jnp.float32)
    order_col = order_f[:, None]

    def advance(state_carry, degree):
        before, current, scale_log = state_carry
        degree_f = degree.astype(jnp.float32)
        alpha_term = jnp.sqrt(
            (4.0 * degree_f * degree_f - 1.0)
            / jnp.maximum(degree_f * degree_f - order_col * order_col, 1.0)
        )
        beta_term = jnp.sqrt(
            jnp.maximum((degree_f - 1.0) ** 2 - order_col * order_col, 0.0)
            / jnp.maximum(4.0 * (degree_f - 1.0) ** 2 - 1.0, 1.0)
        )
        stepped = alpha_term * (cosine[None, :] * current - beta_term * before)
        at_start = order_ids[:, None] == degree
        past_start = order_ids[:, None] < degree
        fresh_value = jnp.where(at_start, 1.0, jnp.where(past_start, stepped, 0.0))
        fresh_log = jnp.where(at_start, start_log, scale_log)
        entry_value = fresh_value * jnp.exp(fresh_log)
        rescale = jnp.where(
            past_start | at_start, jnp.maximum(jnp.abs(fresh_value), jnp.abs(current)), 1.0
        )
        return (
            (current / rescale, fresh_value / rescale, fresh_log + jnp.log(rescale)),
            entry_value,
        )

    degrees = jnp.arange(lat_count, dtype=jnp.int32)
    unused, legendre = lax.scan(advance, (blank_rows, blank_rows, blank_rows), degrees)
    return legendre


def filter_modes(banded, legendre, filter_block, quad_weights):
    coefficients = jnp.einsum(
        "lmj,pmcj->pmcl", legendre, banded * quad_weights[None, None, None, :], precision=highest
    )
    coefficients = coefficients * filter_block[None, None, :, :]
    return jnp.einsum("lmj,pmcl->pmcj", legendre, coefficients, precision=highest)


def wrap_columns(extended):
    return jnp.concatenate([extended[:, :, -1:], extended, extended[:, :, :1]], axis=2)


def depthwise_core(extended, kernel, lat_rows, lon_cols):
    accumulated = jnp.zeros((extended.shape[0], lat_rows, lon_cols), jnp.float32)
    for row_shift in range(3):
        for col_shift in range(3):
            piece = extended[
                :, row_shift : row_shift + lat_rows, col_shift : col_shift + lon_cols
            ].astype(jnp.float32)
            accumulated = accumulated + kernel[3 * row_shift + col_shift][:, None, None] * piece
    return accumulated.astype(jnp.bfloat16)


def channel_mlp(summed_low, norm_gain, weight_in, weight_out):
    summed = summed_low.astype(jnp.float32)
    scale_inv = lax.rsqrt(jnp.mean(summed * summed, axis=0, keepdims=True) + epsilon_norm)
    normed = (summed * scale_inv * norm_gain[:, None]).astype(jnp.bfloat16)
    hidden = lax.dot_general(
        weight_in, normed, (((0,), (0,)), ((), ())), preferred_element_type=jnp.float32
    )
    hidden = jax.nn.gelu(hidden, approximate=False).astype(jnp.bfloat16)
    result = summed + lax.dot_general(
        weight_out, hidden, (((0,), (0,)), ((), ())), preferred_element_type=jnp.float32
    )
    return result.astype(jnp.bfloat16)


def add_three(first, second, third):
    total = first.astype(jnp.float32) + second.astype(jnp.float32) + third.astype(jnp.float32)
    return total.astype(jnp.bfloat16)


def on_device(latent_field, spectral_filter, conv_weight, norm_gain, weight_in, weight_out):
    channels, lat_rows, lon_cols = latent_field.shape
    sector_count = lax.axis_size("lon")
    lat_count = lat_rows * lax.axis_size("lat")
    lon_count = lon_cols * sector_count
    chan_block = channels // sector_count
    spread = lax.all_to_all(latent_field, "lon", split_axis=0, concat_axis=2, tiled=True)
    forward, inverse = fourier_tables(lon_count, lat_count)
    flattened = spread.astype(jnp.float32).reshape(chan_block * lat_rows, lon_count)
    spectrum = lax.dot_general(forward, flattened, (((1,), (1,)), ((), ())), precision=highest)
    spectrum = spectrum.reshape(2, lat_count, chan_block, lat_rows)
    banded = lax.all_to_all(spectrum, "lat", split_axis=1, concat_axis=3, tiled=True)
    order_ids = lax.axis_index("lat") * lat_rows + jnp.arange(lat_rows, dtype=jnp.int32)
    legendre = legendre_rows(order_ids, lat_count)
    synthesized = filter_modes(banded, legendre, spectral_filter, quadrature(lat_count))
    regathered = lax.all_to_all(synthesized, "lat", split_axis=3, concat_axis=1, tiled=True)
    regridded = lax.dot_general(
        regathered.reshape(2 * lat_count, chan_block * lat_rows),
        inverse,
        (((0,), (0,)), ((), ())),
        precision=highest,
    )
    spectral = regridded.reshape(chan_block, lat_rows, lon_count).astype(jnp.bfloat16)
    own_kernel = lax.dynamic_slice_in_dim(
        conv_weight, lax.axis_index("lon") * chan_block, chan_block, 1
    )
    rimmed = with_halo(spread, (("lat", 1),), 1)
    sector_mix = depthwise_core(wrap_columns(rimmed), own_kernel, lat_rows, lon_count)
    sector_sum = add_three(spread, spectral, sector_mix)
    summed = lax.all_to_all(sector_sum, "lon", split_axis=2, concat_axis=0, tiled=True)
    summed = summed.reshape(channels, lat_rows * lon_cols)
    result = channel_mlp(summed, norm_gain, weight_in, weight_out)
    return result.reshape(channels, lat_rows, lon_cols)


def transform_factors(lat_count, lon_count):
    theta = (np.arange(lat_count) + 0.5) * (math.pi / lat_count)
    x, s = (np.cos(theta), np.sin(theta))
    quad = s * (math.pi / lat_count)
    phi = 2.0 * math.pi * np.arange(lon_count) / lon_count
    legendre, cosine, sine, degree, order = ([], [], [], [], [])
    for m in range(lat_count):
        k = np.arange(1, m + 1)
        log_start = 0.5 * (
            np.log((2 * m + 1) / (4 * math.pi)) + np.sum(np.log((2 * k - 1) / (2 * k)))
        )
        before, current = (np.zeros(lat_count), np.exp(log_start + m * np.log(s)))
        for l in range(m, lat_count):
            if l > m:
                a = math.sqrt((4.0 * l * l - 1) / (l * l - m * m))
                b = math.sqrt(((l - 1.0) ** 2 - m * m) / (4.0 * (l - 1) ** 2 - 1))
                before, current = (current, a * (x * current - b * before))
            legendre.append(current)
            cosine.append(np.cos(m * phi))
            sine.append(-np.sin(m * phi))
            degree.append(l)
            order.append(m)
    legendre = np.stack(legendre, 1)
    cosine, sine = (np.stack(cosine, 1), np.stack(sine, 1))
    degree, order = (np.array(degree), np.array(order))
    legendre = np.concatenate([legendre, legendre], 1)
    fourier = np.concatenate([cosine, sine], 1)
    weight = np.where(np.concatenate([order, order]) == 0, 1.0, 2.0)
    select = np.arange(lat_count)[:, None] == np.concatenate([degree, degree])[None, :]
    forward = fourier * (2.0 * math.pi / lon_count)
    f32 = np.float32
    return (
        (legendre * quad[:, None]).astype(f32),
        forward.astype(f32),
        legendre.astype(f32),
        (fourier * weight).astype(f32),
        select.astype(f32),
    )


def full_table(rows, columns, lat_devices, lon_devices):
    width = rows.shape[1]
    rows = jnp.asarray(rows).reshape(lat_devices, 1, -1, 1, width)
    columns = jnp.asarray(columns).reshape(1, lon_devices, 1, -1, width)
    return (rows * columns).astype(jnp.bfloat16).reshape(-1, width)


def whole_sphere(
    lat_devices,
    lon_devices,
    latent_field,
    spectral_filter,
    conv_weight,
    norm_gain,
    weight_in,
    weight_out,
):
    channels, lat_rows, lon_cols = latent_field.shape
    devices = lat_devices * lon_devices
    lat_count, lon_count = (lat_rows * lat_devices, lon_cols * lon_devices)
    points = lat_rows * lon_cols
    own = channels // devices
    me_lat, me_lon = (lax.axis_index("lat"), lax.axis_index("lon"))
    start = (me_lat * lon_devices + me_lon) * own
    axes = ("lat", "lon")
    mine = lax.all_to_all(
        latent_field.reshape(devices, own, points), axes, split_axis=0, concat_axis=0, tiled=True
    )
    rows_f, cols_f, rows_i, cols_i, select = transform_factors(lat_count, lon_count)
    analysis = full_table(rows_f, cols_f, lat_devices, lon_devices)
    synthesis = full_table(rows_i, cols_i, lat_devices, lon_devices)
    filters = lax.all_gather(spectral_filter, "lon", axis=0, tiled=True)
    own_filter = lax.dynamic_slice_in_dim(filters, start, own, 0)
    gain = lax.dot_general(
        own_filter, jnp.asarray(select), (((1,), (0,)), ((), ())), precision=highest
    )
    flat = jnp.transpose(mine, (1, 0, 2)).reshape(own, devices * points)
    coefficients = lax.dot_general(
        flat, analysis, (((1,), (0,)), ((), ())), preferred_element_type=jnp.float32
    )
    coefficients = (coefficients * gain).astype(jnp.bfloat16)
    spectral = lax.dot_general(
        coefficients, synthesis, (((1,), (1,)), ((), ())), preferred_element_type=jnp.float32
    ).astype(jnp.bfloat16)
    spectral = spectral.reshape(own, lat_devices, lon_devices, lat_rows, lon_cols)
    own_kernel = lax.dynamic_slice_in_dim(conv_weight, start, own, 1)
    grid = flat.reshape(own, lat_devices, lon_devices, lat_rows, lon_cols)
    grid = jnp.transpose(grid, (0, 1, 3, 2, 4)).reshape(own, lat_count, lon_count)
    spectral = jnp.transpose(spectral, (0, 1, 3, 2, 4)).reshape(own, lat_count, lon_count)
    rimmed = jnp.pad(grid, ((0, 0), (1, 1), (0, 0)))
    mix = depthwise_core(wrap_columns(rimmed), own_kernel, lat_count, lon_count)
    total = add_three(grid, spectral, mix)
    total = total.reshape(own, lat_devices, lat_rows, lon_devices, lon_cols)
    total = jnp.transpose(total, (1, 3, 0, 2, 4)).reshape(devices, own, points)
    summed = lax.all_to_all(total, axes, split_axis=0, concat_axis=0, tiled=True)
    result = channel_mlp(summed.reshape(channels, points), norm_gain, weight_in, weight_out)
    return result.reshape(channels, lat_rows, lon_cols)


def whole_or_banded(lat_devices, lon_devices, *arguments):
    if arguments[0].shape[0] % (lat_devices * lon_devices) == 0:
        return whole_sphere(lat_devices, lon_devices, *arguments)
    return on_device(*arguments)


def solution(mesh):
    return jax.shard_map(
        functools.partial(whole_or_banded, mesh.shape["lat"], mesh.shape["lon"]),
        mesh=mesh,
        in_specs=(P(None, "lat", "lon"), P("lon", None), P(), P(), P(), P()),
        out_specs=P(None, "lat", "lon"),
        check_vma=False,
    )
```

profile of v0, /device:TPU:0, one launch (start us, length us, event | category | flops | bytes accessed | tf_op | source)
XLA Modules:
  0.0 63.5 jit_solution(10295145786277437358)
XLA Ops:
  0.0 2.3 %reshape.71 = bf16[32,20,64]{1,0,2:T(8,128)(2,1)S(1)} reshape(bf16[640,8,8]{0,2,1:T(8,128)(2,1)} %param.11) | data formatting | bytes 163840 | tf_op jit(solution)/shard_map/reshape | solution.py:239
  2.3 0.7 %copy.75 = bf16[32,20,64]{2,1,0:T(8,128)(2,1)S(1)} copy(bf16[32,20,64]{1,0,2:T(8,128)(2,1)S(1)} %reshape.71) | data formatting | bytes 163840 | tf_op jit(solution)/shard_map/reshape | solution.py:239
  3.0 0.8 %reshape.82 = bf16[32,2,640]{2,1,0:T(2,128)(2,1)} reshape(bf16[32,20,64]{2,1,0:T(8,128)(2,1)S(1)} %copy.75) | data formatting | bytes 163840
  3.8 7.3 %all-to-all-start = ((bf16[32,2,640]{2,1,0:T(2,128)(2,1)}), bf16[32,2,640]{2,1,0:T(2,128)(2,1)S(1)}, u32[]{:S(2)}, u32[]{:S(2)}) async-start(bf16[32,2,640]{2,1,0:T(2,128)(2,1)} %reshape.82), calls=%async_computation | async-start | bytes 163840 | tf_op jit(solution)/shard_map/all_to_all | solution.py:238
  11.1 4.4 %multiply_convert_fusion.1 = bf16[4,8,8,8,1056]{4,3,2,1,0:T(8,128)(2,1)} fusion(f32[8,8,1056]{2,1,0:T(8,128)} %constant.102, f32[4,8,1056]{2,1,0:T(8,128)} %constant.101), kind=kLoop, calls=%fused_computation.1 | loop fusion | flops 4325376 | bytes 4730880 | tf_op jit(solution)/shard_map/convert_element_type | solution.py:217
  15.6 3.4 %multiply_convert_fusion = bf16[4,8,8,8,1056]{4,3,2,1,0:T(8,128)(2,1)} fusion(f32[8,8,1056]{2,1,0:T(8,128)S(1)} %copy-done.2, f32[4,8,1056]{2,1,0:T(8,128)S(1)} %copy-done.3), kind=kLoop, calls=%fused_computation | loop fusion | flops 4325376 | bytes 4730880 | tf_op jit(solution)/shard_map/convert_element_type | solution.py:217
  19.0 14.4 %all-gather = f32[8,80,32]{1,2,0:T(8,128)S(1)} all-gather(f32[1,80,32]{1,2,0:T(8,128)S(1)} %bitcast.133), channel_id=1, replica_groups=mesh['lat'=4,'lon'=8] {'lon'}, dimensions={0}, use_global_device_ids=true | all-gather | bytes 92160 | tf_op jit(solution)/shard_map/all_gather | solution.py:244
  33.5 0.1 reshape.81
  33.6 1.1 %dynamic-slice_bitcast_fusion.8 = (f32[20]{0:T(128)S(1)}, f32[20]{0:T(128)S(1)}, f32[20]{0:T(128)S(1)}, f32[20]{0:T(128)S(1)}, f32[20]{0:T(128)S(1)}, /*index=5*...) fusion(f32[9,640]{1,0:T(8,128)} %param.13, s32[]{:T(128)S(6)} %select_n.4, s32[]{:T(128)S(6)} %add.74, ...), kind=kLoop, calls=%fused_computation.103 | loop fusion | bytes 1476 | tf_op jit(solution)/shard_map/mul | solution.py:115
  34.7 0.2 reshape.83
  34.8 0.3 copy.76
  35.2 0.2 reshape.73
  35.4 3.2 %convolution_bitcast_fusion = f32[20,1056]{1,0:T(8,128)S(1)} fusion(bf16[2048,1056]{1,0:T(8,128)(2,1)} %bitcast.124, bf16[20,2048]{1,0:T(8,128)(2,1)S(1)} %reshape.73), kind=kOutput, calls=%fused_computation.3 | convolution fusion | flops 86507520 | bytes 4491776 | tf_op jit(solution)/shard_map/dot_general | solution.py:250
  38.6 0.4 fusion
  39.0 0.1 copy-done.1
  39.1 1.3 %fusion.1 = f32[20,2048]{1,0:T(8,128)S(1)} fusion(bf16[20,1056]{1,0:T(8,128)(2,1)S(1)} %fusion, bf16[2048,1056]{1,0:T(8,128)(2,1)S(1)} %bitcast.125), kind=kOutput, calls=%fused_computation.6 | convolution fusion | flops 86589440 | bytes 4531456 | tf_op jit(solution)/shard_map/dot_general | solution.py:254
  40.4 0.4 copy.81
  40.8 1.1 %copy.82 = f32[20,4,8,8,8]{0,4,3,2,1:T(8,128)} copy(f32[20,4,8,8,8]{0,4,2,3,1:T(8,128)S(1)} %bitcast.126) | data formatting | bytes 327680 | tf_op jit(solution)/shard_map/convert_element_type | solution.py:134
  41.9 1.7 %copy.83 = f32[20,32,64]{2,1,0:T(8,128)S(1)} copy(f32[20,32,64]{0,2,1:T(8,128)} %bitcast.127) | data formatting | bytes 327680 | tf_op jit(solution)/shard_map/convert_element_type | solution.py:134
  43.6 0.1 copy.77
  43.8 0.4 copy.78
  44.1 0.2 pad_slice_fusion.9
  44.4 1.1 %fusion.6 = bf16[20,32,64]{2,1,0:T(8,128)(2,1)S(1)} fusion(f32[20,32,64]{2,1,0:T(8,128)S(1)} %copy.83, bf16[20,32,64]{2,1,0:T(8,128)(2,1)S(1)} %copy.78, bf16[20,34,64]{2,1,0:T(8,128)(2,1)S(1)} %pad.4, bf16[20,34,1]{2,1,0:T(8,128)(2,1)S(1)} %get-tuple-element.6, bf16[20,34,1]{2,1,0:T(8,128)(2,1)S(1)} %get-tuple-element.5, f32[20]{0:T(128)S(1)} %get-tuple-element.15, ...), kind=kLoop, calls=%fused_computation.16 | loop fusion | flops 2007040 | bytes 1520128 | tf_op jit(solution)/shard_map/convert_element_type | solution.py:135
  45.5 0.4 copy.85
  45.9 0.1 copy.86
  46.0 0.3 copy.87
  46.3 0.1 reshape.84
  46.5 12.9 %all_to_all.10 = bf16[32,2,640]{2,1,0:T(2,128)(2,1)S(1)} all-to-all(bf16[32,2,640]{2,1,0:T(2,128)(2,1)S(1)} %reshape.84), channel_id=1, replica_groups=mesh['lat'=4,'lon'=8] {'lat','lon'}, dimensions={0} | all-to-all | bytes 163840 | tf_op jit(solution)/shard_map/all_to_all | solution.py:267
  59.3 0.2 reshape.85
  59.6 0.1 multiply_reduce_fusion
  59.7 0.1 copy.88
  59.9 3.6 %fusion.4 = bf16[640,8,8]{0,2,1:T(8,128)(2,1)} fusion(f32[640,64]{0,1:T(8,128)S(1)} %copy.88, bf16[1280,640]{1,0:T(8,128)(2,1)S(1)} %copy-done, bf16[640,1280]{1,0:T(8,128)(2,1)} %param.15, f32[640,64]{1,0:T(8,128)S(1)} %reshape.78, f32[640]{0:T(1024)S(1)} %copy-done.6, f32[64]{0:T(128)S(1)} %add_rsqrt_fusion), kind=kOutput, calls=%fused_computation.10 | convolution fusion | flops 215244800 | bytes 3689216 | tf_op jit(solution)/shard_map/dot_general | solution.py:127
  (19 shorter events, 0.3 us)
Async XLA Ops:
  0.0 59.8 %copy-start = (bf16[1280,640]{1,0:T(8,128)(2,1)S(1)}, bf16[1280,640]{1,0:T(8,128)(2,1)}, u32[]{:S(2)}) copy-start(bf16[1280,640]{1,0:T(8,128)(2,1)} %param.16) | copy-start | bytes 4915204
  0.0 15.6 %copy-start.3 = (f32[4,8,1056]{2,1,0:T(8,128)S(1)}, f32[4,8,1056]{2,1,0:T(8,128)}, u32[]{:S(2)}) copy-start(f32[4,8,1056]{2,1,0:T(8,128)} %constant.103) | copy-start | bytes 405508
  0.0 15.6 %copy-start.2 = (f32[8,8,1056]{2,1,0:T(8,128)S(1)}, f32[8,8,1056]{2,1,0:T(8,128)}, u32[]{:S(2)}) copy-start(f32[8,8,1056]{2,1,0:T(8,128)} %constant.104) | copy-start | bytes 811012
  3.8 30.9 %all-to-all-start = ((bf16[32,2,640]{2,1,0:T(2,128)(2,1)}), bf16[32,2,640]{2,1,0:T(2,128)(2,1)S(1)}, u32[]{:S(2)}, u32[]{:S(2)}) async-start(bf16[32,2,640]{2,1,0:T(2,128)(2,1)} %reshape.82), calls=%async_computation | async-start | bytes 163840 | tf_op jit(solution)/shard_map/all_to_all | solution.py:238
  11.1 7.9 %copy-start.5 = (f32[80,32]{0,1:T(8,128)S(1)}, f32[80,32]{0,1:T(8,128)}, u32[]{:S(2)}) copy-start(f32[80,32]{0,1:T(8,128)} %param.12) | copy-start | bytes 30724
  19.0 19.6 %copy-start.4 = (f32[32,1056]{1,0:T(8,128)S(1)}, f32[32,1056]{1,0:T(8,128)}, u32[]{:S(2)}) copy-start(f32[32,1056]{1,0:T(8,128)} %constant.98.clone) | copy-start | bytes 405508
  35.4 3.8 %copy-start.1 = (bf16[4,8,8,8,1056]{4,3,2,1,0:T(8,128)(2,1)S(1)}, bf16[4,8,8,8,1056]{4,3,2,1,0:T(8,128)(2,1)}, u32[]{:S(2)}) copy-start(bf16[4,8,8,8,1056]{4,3,2,1,0:T(8,128)(2,1)} %multiply_convert_fusion) | copy-start | bytes 12976132
  41.9 17.9 %copy-start.6 = (f32[640]{0:T(1024)S(1)}, f32[640]{0:T(1024)}, u32[]{:S(2)}) copy-start(f32[640]{0:T(1024)} %param.14) | copy-start | bytes 7684
where the time goes:
time: 63.8 us; the launch traced here: 63.5 us
  blocking collectives  27.3 us (43%)
  local copies, waits for them, and re-layouts  11 us (17%)
  other arithmetic  9.14 us (14%)
  matrix products  8.54 us (13%)
  starting transfers between devices  7.33 us (11%)
    all_gather x1, blocking collectives, whole_sphere(): filters = lax.all_gather(spectral_filter, 'lon', axis=0, tiled=True)  14.4 us
    all_to_all x1, blocking collectives, whole_sphere(): lax.all_to_all(total, axes, split_axis=0, concat_axis=0, tiled=True)  12.9 us
    convert_element_type x2, other arithmetic, full_table(): return (rows * columns).astype(jnp.bfloat16).reshape(-1, width)  7.86 us
    all_to_all x1, starting transfers between devices, whole_sphere(): lax.all_to_all(latent_field.reshape(devices, own, points), axes, split_ax...  7.33 us
    dot_general x1, matrix products, channel_mlp(): lax.dot_general(weight_out, hidden, (((0,), (0,)), ((), ())), preferred_e...  3.62 us
    dot_general x1, matrix products, whole_sphere(): lax.dot_general(flat, analysis, (((1,), (0,)), ((), ())), preferred_eleme...  3.21 us
    convert_element_type x3, local copies, waits for them, and re-layouts, add_three(): second.astype(jnp.float32)  3.16 us
    reshape x2, local copies, waits for them, and re-layouts, whole_sphere(): latent_field.reshape(devices, own, points)  2.95 us
  transfers between devices with their start and end apart: 1, of which 0 were waited for; matrix products, arithmetic and copies ran while one was open for 14% of the time, Pallas kernels for 0%

commit v1 on v0

--- a/solution.py
+++ b/solution.py
@@ -241,7 +241,15 @@
     rows_f, cols_f, rows_i, cols_i, select = transform_factors(lat_count, lon_count)
     analysis = full_table(rows_f, cols_f, lat_devices, lon_devices)
     synthesis = full_table(rows_i, cols_i, lat_devices, lon_devices)
-    filters = lax.all_gather(spectral_filter, "lon", axis=0, tiled=True)
+    slots = lax.psum(1, "lon")
+    small = [(j - 1, j) for j in range(1, slots)] + [(slots - 1, 0)]
+    tmp = spectral_filter
+    arrivals = [tmp]
+    for _ in [*range(slots - 1)]:
+        tmp = lax.ppermute(tmp, "lon", small)
+        arrivals += [tmp]
+    opened = jnp.concatenate([*reversed(arrivals)], axis=0)
+    filters = jnp.roll(opened, (lax.axis_index("lon") + 1) * tmp.shape[0], axis=0)
     own_filter = lax.dynamic_slice_in_dim(filters, start, own, 0)
     gain = lax.dot_general(
         own_filter, jnp.asarray(select), (((1,), (0,)), ((), ())), precision=highest

time: 63.8 us -> 68.3 us (1.071)
  waiting for transfers between devices: 0.01 us -> 21.4 us
  blocking collectives: 27.3 us -> 10.1 us
    ppermute x0 -> x7, waiting for transfers between devices: none -> 21.4 us  [whole_sphere(): tmp = lax.ppermute(tmp, 'lon', small)]
    all_gather x1 -> x0, blocking collectives: 14.4 us -> none  [whole_sphere(): filters = lax.all_gather(spectral_filter, 'lon', axis=0, tiled=True)]
    all_to_all x1, blocking collectives: 12.9 us -> 10.1 us  [whole_sphere(): lax.all_to_all(total, axes, split_axis=0, concat_axis=0, tiled=True)]
    ppermute x0 -> x7, starting transfers between devices: none -> 1.48 us  [whole_sphere(): tmp = lax.ppermute(tmp, 'lon', small)]
    all_to_all x1, starting transfers between devices: 7.33 us -> 6.28 us  [whole_sphere(): lax.all_to_all(latent_field.reshape(devices, own, points), axes, split_ax...]
    unnamed x19 -> x18, local copies, waits for them, and re-layouts: 1.52 us -> 1.42 us
  transfers between devices with their start and end apart: 1 -> 8, of which waited for: 0 -> 6; matrix products, arithmetic and copies ran while one was open for 14% -> 19% of each run, Pallas kernels for 0% -> 0%
where the time goes in v1:
time: 68.3 us; the launch traced here: 68 us
  waiting for transfers between devices  21.4 us (31%)
  local copies, waits for them, and re-layouts  10.8 us (16%)
  blocking collectives  10.1 us (15%)
  other arithmetic  9.12 us (13%)
  matrix products  8.55 us (13%)
  starting transfers between devices  7.76 us (11%)
    ppermute x7, waiting for transfers between devices, whole_sphere(): tmp = lax.ppermute(tmp, 'lon', small)  21.4 us
    all_to_all x1, blocking collectives, whole_sphere(): lax.all_to_all(total, axes, split_axis=0, concat_axis=0, tiled=True)  10.1 us
    convert_element_type x2, other arithmetic, full_table(): return (rows * columns).astype(jnp.bfloat16).reshape(-1, width)  7.85 us
    all_to_all x1, starting transfers between devices, whole_sphere(): lax.all_to_all(latent_field.reshape(devices, own, points), axes, split_ax...  6.28 us
    dot_general x1, matrix products, channel_mlp(): lax.dot_general(weight_out, hidden, (((0,), (0,)), ((), ())), preferred_e...  3.62 us
    dot_general x1, matrix products, whole_sphere(): lax.dot_general(flat, analysis, (((1,), (0,)), ((), ())), preferred_eleme...  3.21 us
    convert_element_type x3, local copies, waits for them, and re-layouts, add_three(): second.astype(jnp.float32)  3.17 us
    reshape x2, local copies, waits for them, and re-layouts, whole_sphere(): latent_field.reshape(devices, own, points)  2.81 us
  transfers between devices with their start and end apart: 8, of which 6 were waited for; matrix products, arithmetic and copies ran while one was open for 19% of the time, Pallas kernels for 0%

profile of v1, /device:TPU:0, one launch (start us, length us, event | category | flops | bytes accessed | tf_op | source)
XLA Modules:
  0.0 68.0 jit_solution(6061464414055936667)
XLA Ops:
  0.0 0.6 collective-permute-start
  0.6 5.7 %collective-permute-done = f32[80,32]{0,1:T(8,128)S(1)} collective-permute-done((f32[80,32]{0,1:T(8,128)}, f32[80,32]{0,1:T(8,128)S(1)}, u32[]{:S(2)}, u32[]{:S(2)}) %collective-permute-start) | collective-permute-done | bytes 10272 | tf_op jit(solution)/shard_map/ppermute | solution.py:249
  6.2 5.0 %collective-permute-done.1 = f32[80,32]{0,1:T(8,128)S(1)} collective-permute-done((f32[80,32]{0,1:T(8,128)S(1)}, f32[80,32]{0,1:T(8,128)S(1)}, u32[]{:S(2)}, u32[]{:S(2)}) %collective-permute-start.1) | collective-permute-done | bytes 10272 | tf_op jit(solution)/shard_map/ppermute | solution.py:249
  11.2 5.0 %collective-permute-done.2 = f32[80,32]{0,1:T(8,128)S(1)} collective-permute-done((f32[80,32]{0,1:T(8,128)S(1)}, f32[80,32]{0,1:T(8,128)S(1)}, u32[]{:S(2)}, u32[]{:S(2)}) %collective-permute-start.2) | collective-permute-done | bytes 10272 | tf_op jit(solution)/shard_map/ppermute | solution.py:249
  16.1 2.1 %reshape.71 = bf16[32,20,64]{1,0,2:T(8,128)(2,1)S(1)} reshape(bf16[640,8,8]{0,2,1:T(8,128)(2,1)} %param.11) | data formatting | bytes 163840 | tf_op jit(solution)/shard_map/reshape | solution.py:239
  18.3 0.7 copy.70
  19.0 0.8 %reshape.80 = bf16[32,2,640]{2,1,0:T(2,128)(2,1)} reshape(bf16[32,20,64]{2,1,0:T(8,128)(2,1)S(1)} %copy.70) | data formatting | bytes 163840
  19.7 6.3 %all-to-all-start = ((bf16[32,2,640]{2,1,0:T(2,128)(2,1)}), bf16[32,2,640]{2,1,0:T(2,128)(2,1)S(1)}, u32[]{:S(2)}, u32[]{:S(2)}) async-start(bf16[32,2,640]{2,1,0:T(2,128)(2,1)} %reshape.80), calls=%async_computation | async-start | bytes 163840 | tf_op jit(solution)/shard_map/all_to_all | solution.py:238
  26.1 0.3 collective-permute-start.4
  26.4 4.4 %multiply_convert_fusion.1 = bf16[4,8,8,8,1056]{4,3,2,1,0:T(8,128)(2,1)} fusion(f32[8,8,1056]{2,1,0:T(8,128)} %constant.133, f32[4,8,1056]{2,1,0:T(8,128)} %constant.132), kind=kLoop, calls=%fused_computation.1 | loop fusion | flops 4325376 | bytes 4730880 | tf_op jit(solution)/shard_map/convert_element_type | solution.py:217
  30.8 1.0 %collective-permute-done.4 = f32[80,32]{0,1:T(8,128)S(1)} collective-permute-done((f32[80,32]{0,1:T(8,128)S(1)}, f32[80,32]{0,1:T(8,128)S(1)}, u32[]{:S(2)}, u32[]{:S(2)}) %collective-permute-start.4) | collective-permute-done | bytes 10272 | tf_op jit(solution)/shard_map/ppermute | solution.py:249
  31.8 0.6 collective-permute-start.5
  32.4 3.4 %multiply_convert_fusion = bf16[4,8,8,8,1056]{4,3,2,1,0:T(8,128)(2,1)} fusion(f32[8,8,1056]{2,1,0:T(8,128)S(1)} %copy-done.2, f32[4,8,1056]{2,1,0:T(8,128)S(1)} %copy-done.3), kind=kLoop, calls=%fused_computation | loop fusion | flops 4325376 | bytes 4730880 | tf_op jit(solution)/shard_map/convert_element_type | solution.py:217
  35.9 0.9 %collective-permute-done.5 = f32[80,32]{0,1:T(8,128)S(1)} collective-permute-done((f32[80,32]{0,1:T(8,128)S(1)}, f32[80,32]{0,1:T(8,128)S(1)}, u32[]{:S(2)}, u32[]{:S(2)}) %collective-permute-start.5) | collective-permute-done | bytes 10272 | tf_op jit(solution)/shard_map/ppermute | solution.py:249
  36.8 1.1 %dynamic-slice_bitcast_fusion.8 = (f32[20]{0:T(128)S(1)}, f32[20]{0:T(128)S(1)}, f32[20]{0:T(128)S(1)}, f32[20]{0:T(128)S(1)}, f32[20]{0:T(128)S(1)}, /*index=5*...) fusion(f32[9,640]{1,0:T(8,128)} %param.13, s32[]{:T(128)S(6)} %select_n.21, s32[]{:T(128)S(6)} %add.92, ...), kind=kLoop, calls=%fused_computation.103 | loop fusion | bytes 1476 | tf_op jit(solution)/shard_map/mul | solution.py:115
  37.9 3.9 %collective-permute-done.6 = f32[80,32]{0,1:T(8,128)S(1)} collective-permute-done((f32[80,32]{0,1:T(8,128)S(1)}, f32[80,32]{0,1:T(8,128)S(1)}, u32[]{:S(2)}, u32[]{:S(2)}) %collective-permute-start.6) | collective-permute-done | bytes 10272 | tf_op jit(solution)/shard_map/ppermute | solution.py:249
  41.9 0.2 reshape.81
  42.1 0.3 copy.71
  42.4 0.2 reshape.73
  42.6 3.2 %convolution_bitcast_fusion = f32[20,1056]{1,0:T(8,128)S(1)} fusion(bf16[2048,1056]{1,0:T(8,128)(2,1)} %bitcast.121, bf16[20,2048]{1,0:T(8,128)(2,1)S(1)} %reshape.73), kind=kOutput, calls=%fused_computation.3 | convolution fusion | flops 86507520 | bytes 4491776 | tf_op jit(solution)/shard_map/dot_general | solution.py:258
  45.8 0.4 fusion
  46.4 1.3 %fusion.1 = f32[20,2048]{1,0:T(8,128)S(1)} fusion(bf16[20,1056]{1,0:T(8,128)(2,1)S(1)} %fusion, bf16[2048,1056]{1,0:T(8,128)(2,1)S(1)} %bitcast.122), kind=kOutput, calls=%fused_computation.6 | convolution fusion | flops 86589440 | bytes 4531456 | tf_op jit(solution)/shard_map/dot_general | solution.py:262
  47.7 0.4 copy.75
  48.1 1.1 %copy.76 = f32[20,4,8,8,8]{0,4,3,2,1:T(8,128)} copy(f32[20,4,8,8,8]{0,4,2,3,1:T(8,128)S(1)} %bitcast.123) | data formatting | bytes 327680 | tf_op jit(solution)/shard_map/convert_element_type | solution.py:134
  49.2 1.7 %copy.77 = f32[20,32,64]{2,1,0:T(8,128)S(1)} copy(f32[20,32,64]{0,2,1:T(8,128)} %bitcast.124) | data formatting | bytes 327680 | tf_op jit(solution)/shard_map/convert_element_type | solution.py:134
  51.0 0.4 copy.73
  51.6 1.1 %fusion.6 = bf16[20,32,64]{2,1,0:T(8,128)(2,1)S(1)} fusion(f32[20,32,64]{2,1,0:T(8,128)S(1)} %copy.77, bf16[20,32,64]{2,1,0:T(8,128)(2,1)S(1)} %copy.73, bf16[20,34,64]{2,1,0:T(8,128)(2,1)S(1)} %pad.4, bf16[20,34,1]{2,1,0:T(8,128)(2,1)S(1)} %get-tuple-element.6, bf16[20,34,1]{2,1,0:T(8,128)(2,1)S(1)} %get-tuple-element.5, f32[20]{0:T(128)S(1)} %get-tuple-element.15, ...), kind=kLoop, calls=%fused_computation.16 | loop fusion | flops 2007040 | bytes 1520128 | tf_op jit(solution)/shard_map/convert_element_type | solution.py:135
  52.8 0.4 copy.79
  53.3 0.3 copy.81
  53.7 10.1 %all_to_all.10 = bf16[32,2,640]{2,1,0:T(2,128)(2,1)S(1)} all-to-all(bf16[32,2,640]{2,1,0:T(2,128)(2,1)S(1)} %reshape.82), channel_id=1, replica_groups=mesh['lat'=4,'lon'=8] {'lat','lon'}, dimensions={0} | all-to-all | bytes 163840 | tf_op jit(solution)/shard_map/all_to_all | solution.py:275
  63.9 0.2 reshape.83
  64.4 3.6 %fusion.4 = bf16[640,8,8]{0,2,1:T(8,128)(2,1)} fusion(f32[640,64]{0,1:T(8,128)S(1)} %copy.82, bf16[1280,640]{1,0:T(8,128)(2,1)S(1)} %copy-done, bf16[640,1280]{1,0:T(8,128)(2,1)} %param.15, f32[640,64]{1,0:T(8,128)S(1)} %reshape.78, f32[640]{0:T(1024)S(1)} %copy-done.6, f32[64]{0:T(128)S(1)} %add_rsqrt_fusion), kind=kOutput, calls=%fused_computation.10 | convolution fusion | flops 215244800 | bytes 3689216 | tf_op jit(solution)/shard_map/dot_general | solution.py:127
  (31 shorter events, 1.3 us)
Async XLA Ops:
  0.0 64.4 %copy-start = (bf16[1280,640]{1,0:T(8,128)(2,1)S(1)}, bf16[1280,640]{1,0:T(8,128)(2,1)}, u32[]{:S(2)}) copy-start(bf16[1280,640]{1,0:T(8,128)(2,1)} %param.16) | copy-start | bytes 4915204
  0.0 32.4 %copy-start.3 = (f32[4,8,1056]{2,1,0:T(8,128)S(1)}, f32[4,8,1056]{2,1,0:T(8,128)}, u32[]{:S(2)}) copy-start(f32[4,8,1056]{2,1,0:T(8,128)} %constant.134) | copy-start | bytes 405508
  0.0 32.4 %copy-start.2 = (f32[8,8,1056]{2,1,0:T(8,128)S(1)}, f32[8,8,1056]{2,1,0:T(8,128)}, u32[]{:S(2)}) copy-start(f32[8,8,1056]{2,1,0:T(8,128)} %constant.135) | copy-start | bytes 811012
  0.0 6.2 %collective-permute-start = (f32[80,32]{0,1:T(8,128)}, f32[80,32]{0,1:T(8,128)S(1)}, u32[]{:S(2)}, u32[]{:S(2)}) collective-permute-start(f32[80,32]{0,1:T(8,128)} %param.12), channel_id=1, source_target_pairs={{0,1},{1,2},{2,3},{3,4},{4,5},{5,6},{6,7},{7,0},{8,9},{9,10},{10,1... | collective-permute-start | bytes 30728 | tf_op jit(solution)/shard_map/ppermute | solution.py:249
  6.2 5.0 %collective-permute-start.1 = (f32[80,32]{0,1:T(8,128)S(1)}, f32[80,32]{0,1:T(8,128)S(1)}, u32[]{:S(2)}, u32[]{:S(2)}) collective-permute-start(f32[80,32]{0,1:T(8,128)S(1)} %collective-permute-done), channel_id=1, source_target_pairs={{0,1},{1,2},{2,3},{3,4},{4,5},{5,6},{6,7},{7,0},{8,9},{9,10},{10,1... | collective-permute-start | bytes 30728 | tf_op jit(solution)/shard_map/ppermute | solution.py:249
  11.2 5.0 %collective-permute-start.2 = (f32[80,32]{0,1:T(8,128)S(1)}, f32[80,32]{0,1:T(8,128)S(1)}, u32[]{:S(2)}, u32[]{:S(2)}) collective-permute-start(f32[80,32]{0,1:T(8,128)S(1)} %collective-permute-done.1), channel_id=1, source_target_pairs={{0,1},{1,2},{2,3},{3,4},{4,5},{5,6},{6,7},{7,0},{8,9},{9,10},{10,1... | collective-permute-start | bytes 30728 | tf_op jit(solution)/shard_map/ppermute | solution.py:249
  16.1 9.9 %collective-permute-start.3 = (f32[80,32]{0,1:T(8,128)S(1)}, f32[80,32]{0,1:T(8,128)S(1)}, u32[]{:S(2)}, u32[]{:S(2)}) collective-permute-start(f32[80,32]{0,1:T(8,128)S(1)} %collective-permute-done.2), channel_id=1, source_target_pairs={{0,1},{1,2},{2,3},{3,4},{4,5},{5,6},{6,7},{7,0},{8,9},{9,10},{10,1... | collective-permute-start | bytes 30728 | tf_op jit(solution)/shard_map/ppermute | solution.py:249
  19.7 22.2 %all-to-all-start = ((bf16[32,2,640]{2,1,0:T(2,128)(2,1)}), bf16[32,2,640]{2,1,0:T(2,128)(2,1)S(1)}, u32[]{:S(2)}, u32[]{:S(2)}) async-start(bf16[32,2,640]{2,1,0:T(2,128)(2,1)} %reshape.80), calls=%async_computation | async-start | bytes 163840 | tf_op jit(solution)/shard_map/all_to_all | solution.py:238
  26.0 15.7 %copy-start.5 = (f32[80,32]{0,1:T(8,128)S(1)}, f32[80,32]{0,1:T(8,128)}, u32[]{:S(2)}) copy-start(f32[80,32]{0,1:T(8,128)} %param.12) | copy-start | bytes 30724
  26.1 5.8 %collective-permute-start.4 = (f32[80,32]{0,1:T(8,128)S(1)}, f32[80,32]{0,1:T(8,128)S(1)}, u32[]{:S(2)}, u32[]{:S(2)}) collective-permute-start(f32[80,32]{0,1:T(8,128)S(1)} %collective-permute-done.3), channel_id=1, source_target_pairs={{0,1},{1,2},{2,3},{3,4},{4,5},{5,6},{6,7},{7,0},{8,9},{9,10},{10,1... | collective-permute-start | bytes 30728 | tf_op jit(solution)/shard_map/ppermute | solution.py:249
  31.8 5.0 %collective-permute-start.5 = (f32[80,32]{0,1:T(8,128)S(1)}, f32[80,32]{0,1:T(8,128)S(1)}, u32[]{:S(2)}, u32[]{:S(2)}) collective-permute-start(f32[80,32]{0,1:T(8,128)S(1)} %collective-permute-done.4), channel_id=1, source_target_pairs={{0,1},{1,2},{2,3},{3,4},{4,5},{5,6},{6,7},{7,0},{8,9},{9,10},{10,1... | collective-permute-start | bytes 30728 | tf_op jit(solution)/shard_map/ppermute | solution.py:249
  35.9 10.0 %copy-start.4 = (f32[32,1056]{1,0:T(8,128)S(1)}, f32[32,1056]{1,0:T(8,128)}, u32[]{:S(2)}) copy-start(f32[32,1056]{1,0:T(8,128)} %constant.129.clone) | copy-start | bytes 405508
  36.8 5.0 %collective-permute-start.6 = (f32[80,32]{0,1:T(8,128)S(1)}, f32[80,32]{0,1:T(8,128)S(1)}, u32[]{:S(2)}, u32[]{:S(2)}) collective-permute-start(f32[80,32]{0,1:T(8,128)S(1)} %collective-permute-done.5), channel_id=1, source_target_pairs={{0,1},{1,2},{2,3},{3,4},{4,5},{5,6},{6,7},{7,0},{8,9},{9,10},{10,1... | collective-permute-start | bytes 30728 | tf_op jit(solution)/shard_map/ppermute | solution.py:249
  42.6 3.8 %copy-start.1 = (bf16[4,8,8,8,1056]{4,3,2,1,0:T(8,128)(2,1)S(1)}, bf16[4,8,8,8,1056]{4,3,2,1,0:T(8,128)(2,1)}, u32[]{:S(2)}) copy-start(bf16[4,8,8,8,1056]{4,3,2,1,0:T(8,128)(2,1)} %multiply_convert_fusion) | copy-start | bytes 12976132
  49.2 15.2 %copy-start.6 = (f32[640]{0:T(1024)S(1)}, f32[640]{0:T(1024)}, u32[]{:S(2)}) copy-start(f32[640]{0:T(1024)} %param.14) | copy-start | bytes 7684
